TPU v7x, 32 devices: a whole 2x2x4 slice. The times are simulated.
32 devices in a mesh: dp: 8 (over z, core), tensor: 4 (over y, x).
Axes of the slice: x: 2, y: 2, z: 4, core: 2. Of those that a mesh axis runs over, the one named last changes fastest.
Arguments:
- block_input: bfloat16 [8192, 2048], P(('dp', 'tensor')), may hold values from -6 to 6
- attn_gain: float32 [2048], replicated, may hold values from 0.5 to 1.5
- w_query: bfloat16 [2048, 2048], P('dp', 'tensor'), may hold values from -6 to 6
- w_key: bfloat16 [2048, 512], P('dp', 'tensor'), may hold values from -0.125 to 0.125
- w_value: bfloat16 [2048, 512], P('dp', 'tensor'), may hold values from -0.125 to 0.125
- w_out: bfloat16 [2048, 2048], P('dp', 'tensor'), may hold values from -0.5 to 0.5
- mlp_gain: float32 [2048], replicated, may hold values from 0.5 to 1.5
- w_gate: bfloat16 [2048, 8192], P('dp', 'tensor'), may hold values from -0.125 to 0.125
- w_up: bfloat16 [2048, 8192], P('dp', 'tensor'), may hold values from -0.125 to 0.125
- w_down: bfloat16 [2048, 8192], P('dp', 'tensor'), may hold values from -0.0625 to 0.0625
- doc_ids: int32 [8192], P('dp'), may hold values from -1 to 3, as said below
- cotangent: bfloat16 [8192, 2048], P(('dp', 'tensor')), may hold values from -6 to 6
Outputs:
- block_output: bfloat16 [8192, 2048], P(('dp', 'tensor'))
- input_grad: bfloat16 [8192, 2048], P(('dp', 'tensor'))
- grad_query: float32 [2048, 2048], P('dp', 'tensor')
- grad_key: float32 [2048, 512], P('dp', 'tensor')
- grad_value: float32 [2048, 512], P('dp', 'tensor')
- grad_out: float32 [2048, 2048], P('dp', 'tensor')
- grad_gate: float32 [2048, 8192], P('dp', 'tensor')
- grad_up: float32 [2048, 8192], P('dp', 'tensor')
- grad_down: float32 [2048, 8192], P('dp', 'tensor')
- grad_attn_gain: float32 [2048], replicated
- grad_mlp_gain: float32 [2048], replicated
Inputs may be any that keep to these rules, and one draw needn't show every extreme that they name: `doc_ids`: within each aligned block of 512 positions the ids of live positions never fall; -1 marks padding, which only ends a block; a block whose first position is -1 is padding throughout; every block ends with padding; a live block has at least 256 live positions; some index of dp has all its 2 blocks live, others may have fewer.
All inputs are finite; a program needn't handle non-finite values.
Results may differ from a plain program's by a relative error of at most 0.014.
The roundings to bfloat16 on the way count: a program that leaves them out, or rounds other values in their place, can miss the bound.
Values may be sent and summed in bfloat16 or wider, within the bound.
A program may use at most 256 MiB of HBM per device.

v0:
```python
import jax
import jax.numpy as jnp
from jax import lax
from jax.sharding import PartitionSpec as P

HD = 64
SEQ = 512
EPSILON = 1e-05
ROPE_BASE = 500000.0
NEG_LARGE = -1e30


def rotary_tables(length, head_dim):
    half_dim = head_dim // 2
    frequency = ROPE_BASE ** (-(jnp.arange(half_dim, dtype=jnp.float32) * (2.0 / head_dim)))
    angles = jnp.arange(length, dtype=jnp.float32)[:, None] * frequency[None, :]
    angles = jnp.concatenate([angles, angles], axis=1)
    return (jnp.cos(angles), jnp.sin(angles))


def rotate_half(tensor_rows):
    half_dim = tensor_rows.shape[-1] // 2
    return jnp.concatenate([-tensor_rows[..., half_dim:], tensor_rows[..., :half_dim]], axis=-1)


def rotate_back(tensor_rows):
    half_dim = tensor_rows.shape[-1] // 2
    return jnp.concatenate([tensor_rows[..., half_dim:], -tensor_rows[..., :half_dim]], axis=-1)


def apply_rotary(tensor_rows, cosine_table, sine_table):
    return (
        tensor_rows * cosine_table[:, None, :] + rotate_half(tensor_rows) * sine_table[:, None, :]
    )


def undo_rotary(tensor_rows, cosine_table, sine_table):
    return tensor_rows * cosine_table[:, None, :] + rotate_back(
        tensor_rows * sine_table[:, None, :]
    )


def norm_scale(tensor_rows):
    return lax.rsqrt(jnp.mean(tensor_rows * tensor_rows, axis=1, keepdims=True) + EPSILON)


def norm_back(grad_normed, tensor_rows, row_scale, gain_row):
    weighted = grad_normed * gain_row[None, :]
    inner_mean = jnp.mean(weighted * tensor_rows, axis=1, keepdims=True)
    return row_scale * weighted - tensor_rows * (row_scale * row_scale * row_scale) * inner_mean


def slot_mask(doc_rows):
    positions = jnp.arange(doc_rows.shape[0])
    earlier = positions[None, :] <= positions[:, None]
    same_doc = (doc_rows[:, None] == doc_rows[None, :]) & (doc_rows[:, None] >= 0)
    return same_doc & earlier | (positions[None, :] == positions[:, None])


def contract_rows(left_side, right_side):
    return lax.dot_general(
        left_side, right_side, (((0,), (0,)), ((), ())), preferred_element_type=jnp.float32
    )


def contract_cols(left_side, right_side):
    return lax.dot_general(
        left_side, right_side, (((1,), (1,)), ((), ())), preferred_element_type=jnp.float32
    )


def slot_scores(query_rows, key_rows, allowed):
    seq_len, head_count, head_dim = query_rows.shape
    groups = key_rows.shape[1]
    grouped = query_rows.reshape(seq_len, groups, head_count // groups, head_dim)
    scores = jnp.einsum(
        "sgjd,tgd->gjst", grouped, key_rows, preferred_element_type=jnp.float32
    ) * head_dim ** (-0.5)
    return (grouped, jnp.where(allowed[None, None], scores, NEG_LARGE))


def attend(packed):
    query_rows, key_rows, value_rows, doc_rows = packed
    seq_len, head_count, head_dim = query_rows.shape
    allowed = slot_mask(doc_rows)
    live_rows = (doc_rows >= 0).astype(jnp.float32)
    grouped, scores = slot_scores(query_rows, key_rows, allowed)
    row_max = jnp.max(scores, axis=-1, keepdims=True)
    weights = jnp.exp(scores - row_max)
    row_total = jnp.sum(weights, axis=-1, keepdims=True)
    prob_bf = (weights / row_total).astype(jnp.bfloat16)
    mixed_rows = jnp.einsum(
        "gjst,tgd->sgjd", prob_bf, value_rows, preferred_element_type=jnp.float32
    )
    mixed_rows = mixed_rows.reshape(seq_len, head_count * head_dim) * live_rows[:, None]
    return (mixed_rows.astype(jnp.bfloat16), row_max + jnp.log(row_total))


def attend_back(packed):
    query_rows, key_rows, value_rows, doc_rows, log_total, grad_mixed = packed
    seq_len, head_count, head_dim = query_rows.shape
    groups = key_rows.shape[1]
    allowed = slot_mask(doc_rows)
    grouped, scores = slot_scores(query_rows, key_rows, allowed)
    prob_full = jnp.where(allowed[None, None], jnp.exp(scores - log_total), 0.0)
    grad_rows = grad_mixed.reshape(seq_len, groups, head_count // groups, head_dim)
    grad_prob = jnp.einsum(
        "sgjd,tgd->gjst", grad_rows, value_rows, preferred_element_type=jnp.float32
    )
    row_delta = jnp.sum(prob_full * grad_prob, axis=-1, keepdims=True)
    grad_scores = (prob_full * (grad_prob - row_delta)).astype(jnp.bfloat16)
    grad_values = jnp.einsum(
        "gjst,sgjd->tgd",
        prob_full.astype(jnp.bfloat16),
        grad_rows,
        preferred_element_type=jnp.float32,
    )
    grad_queries = jnp.einsum(
        "gjst,tgd->sgjd", grad_scores, key_rows, preferred_element_type=jnp.float32
    ) * head_dim ** (-0.5)
    grad_keys = jnp.einsum(
        "gjst,sgjd->tgd", grad_scores, grouped, preferred_element_type=jnp.float32
    ) * head_dim ** (-0.5)
    return (grad_queries.reshape(seq_len, head_count, head_dim), grad_keys, grad_values)


def sum_rows(partial, axis):
    return lax.psum_scatter(
        partial.astype(jnp.bfloat16), axis, scatter_dimension=0, tiled=True
    ).astype(jnp.float32)


def per_device(
    block_input,
    attn_gain,
    w_query,
    w_key,
    w_value,
    w_out,
    mlp_gain,
    w_gate,
    w_up,
    w_down,
    doc_ids,
    cotangent,
):
    query_full, key_full, value_full, out_full, gate_full, up_full, down_full = (
        lax.all_gather(w_query, "dp", axis=0, tiled=True),
        lax.all_gather(w_key, "dp", axis=0, tiled=True),
        lax.all_gather(w_value, "dp", axis=0, tiled=True),
        lax.all_gather(w_out, "dp", axis=0, tiled=True),
        lax.all_gather(w_gate, "dp", axis=0, tiled=True),
        lax.all_gather(w_up, "dp", axis=0, tiled=True),
        lax.all_gather(w_down, "dp", axis=0, tiled=True),
    )
    total_rows = doc_ids.shape[0]
    slot_count = total_rows // SEQ
    local_heads = query_full.shape[1] // HD
    local_groups = key_full.shape[1] // HD
    cosine_table, sine_table = rotary_tables(SEQ, HD)
    live_all = (doc_ids >= 0).astype(jnp.float32)
    input_own = block_input.astype(jnp.float32)
    scale_one = norm_scale(input_own)
    normed_one = lax.all_gather(
        (input_own * scale_one * attn_gain[None, :]).astype(jnp.bfloat16),
        "tensor",
        axis=0,
        tiled=True,
    )
    query_pre = jnp.dot(normed_one, query_full, preferred_element_type=jnp.float32).reshape(
        slot_count, SEQ, local_heads, HD
    )
    key_pre = jnp.dot(normed_one, key_full, preferred_element_type=jnp.float32).reshape(
        slot_count, SEQ, local_groups, HD
    )
    query_rows = apply_rotary(query_pre, cosine_table, sine_table).astype(jnp.bfloat16)
    key_rows = apply_rotary(key_pre, cosine_table, sine_table).astype(jnp.bfloat16)
    value_rows = (
        jnp.dot(normed_one, value_full, preferred_element_type=jnp.float32)
        .astype(jnp.bfloat16)
        .reshape(slot_count, SEQ, local_groups, HD)
    )
    doc_slots = doc_ids.reshape(slot_count, SEQ)
    mixed_slots, log_total = lax.map(attend, (query_rows, key_rows, value_rows, doc_slots))
    mixed_all = mixed_slots.reshape(total_rows, local_heads * HD)
    residual_own = input_own + sum_rows(contract_cols(mixed_all, out_full), "tensor")
    scale_two_own = norm_scale(residual_own)
    normed_two = lax.all_gather(
        (residual_own * scale_two_own * mlp_gain[None, :]).astype(jnp.bfloat16),
        "tensor",
        axis=0,
        tiled=True,
    )
    gate_pre = jnp.dot(normed_two, gate_full, preferred_element_type=jnp.float32)
    up_pre = jnp.dot(normed_two, up_full, preferred_element_type=jnp.float32)
    sigmoid_gate = jax.nn.sigmoid(gate_pre)
    silu_gate = gate_pre * sigmoid_gate
    hidden = (silu_gate * up_pre).astype(jnp.bfloat16)
    block_output = (residual_own + sum_rows(contract_cols(hidden, down_full), "tensor")).astype(
        jnp.bfloat16
    )
    grad_full = lax.all_gather(cotangent, "tensor", axis=0, tiled=True)
    grad_hidden = jnp.dot(grad_full, down_full, preferred_element_type=jnp.float32)
    grad_down = contract_rows(grad_full, hidden)
    grad_gate_pre = (
        grad_hidden * up_pre * sigmoid_gate * (1.0 + gate_pre * (1.0 - sigmoid_gate))
    ).astype(jnp.bfloat16)
    grad_up_pre = (grad_hidden * silu_gate).astype(jnp.bfloat16)
    grad_gate = contract_rows(normed_two, grad_gate_pre)
    grad_up = contract_rows(normed_two, grad_up_pre)
    grad_normed_own = sum_rows(
        contract_cols(grad_gate_pre, gate_full) + contract_cols(grad_up_pre, up_full), "tensor"
    )
    grad_mlp_gain = jnp.sum(grad_normed_own * residual_own * scale_two_own, axis=0)
    grad_residual_own = cotangent.astype(jnp.float32) + norm_back(
        grad_normed_own, residual_own, scale_two_own, mlp_gain
    )
    grad_residual_bf = lax.all_gather(
        grad_residual_own.astype(jnp.bfloat16), "tensor", axis=0, tiled=True
    )
    grad_out = contract_rows(grad_residual_bf, mixed_all)
    grad_mixed = (
        jnp.dot(grad_residual_bf, out_full, preferred_element_type=jnp.float32) * live_all[:, None]
    ).astype(jnp.bfloat16)
    grad_mixed_slots = grad_mixed.reshape(slot_count, SEQ, local_heads * HD)
    grad_queries, grad_keys, grad_values = lax.map(
        attend_back, (query_rows, key_rows, value_rows, doc_slots, log_total, grad_mixed_slots)
    )
    grad_query_rows = (
        undo_rotary(grad_queries, cosine_table, sine_table)
        .astype(jnp.bfloat16)
        .reshape(total_rows, local_heads * HD)
    )
    grad_key_rows = (
        undo_rotary(grad_keys, cosine_table, sine_table)
        .astype(jnp.bfloat16)
        .reshape(total_rows, local_groups * HD)
    )
    grad_value_rows = grad_values.astype(jnp.bfloat16).reshape(total_rows, local_groups * HD)
    grad_query = contract_rows(normed_one, grad_query_rows)
    grad_key = contract_rows(normed_one, grad_key_rows)
    grad_value = contract_rows(normed_one, grad_value_rows)
    grad_normed_one = sum_rows(
        contract_cols(grad_query_rows, query_full)
        + contract_cols(grad_key_rows, key_full)
        + contract_cols(grad_value_rows, value_full),
        "tensor",
    )
    grad_attn_gain = jnp.sum(grad_normed_one * input_own * scale_one, axis=0)
    input_grad = (
        grad_residual_own + norm_back(grad_normed_one, input_own, scale_one, attn_gain)
    ).astype(jnp.bfloat16)
    summed = (
        sum_rows(grad_query, "dp"),
        sum_rows(grad_key, "dp"),
        sum_rows(grad_value, "dp"),
        sum_rows(grad_out, "dp"),
        sum_rows(grad_gate, "dp"),
        sum_rows(grad_up, "dp"),
        sum_rows(grad_down, "dp"),
    )
    gains = lax.psum((grad_attn_gain, grad_mlp_gain), ("dp", "tensor"))
    return (
        block_output,
        input_grad,
        summed[0],
        summed[1],
        summed[2],
        summed[3],
        summed[4],
        summed[5],
        summed[6],
        gains[0],
        gains[1],
    )


def solution(mesh):
    in_specs = (
        P(("dp", "tensor"), None),
        P(),
        P("dp", "tensor"),
        P("dp", "tensor"),
        P("dp", "tensor"),
        P("dp", "tensor"),
        P(),
        P("dp", "tensor"),
        P("dp", "tensor"),
        P("dp", "tensor"),
        P("dp"),
        P(("dp", "tensor"), None),
    )
    out_specs = (
        P(("dp", "tensor"), None),
        P(("dp", "tensor"), None),
        P("dp", "tensor"),
        P("dp", "tensor"),
        P("dp", "tensor"),
        P("dp", "tensor"),
        P("dp", "tensor"),
        P("dp", "tensor"),
        P("dp", "tensor"),
        P(),
        P(),
    )
    return jax.shard_map(
        per_device, mesh=mesh, in_specs=in_specs, out_specs=out_specs, check_vma=False
    )
```

profile of v0, /device:TPU:0, one launch (start us, length us, event | category | flops | bytes accessed | tf_op | source)
XLA Modules:
  0.0 1358.1 jit_solution(2568812626579666158)
XLA Ops:
  10.7 2.5 fusion.56
  14.4 18.8 %all_gather.35 = bf16[2048,128]{1,0:T(8,128)(2,1)S(1)} all-gather(bf16[256,128]{1,0:T(8,128)(2,1)S(1)} %copy-done.32), channel_id=1, replica_groups=mesh['dp'=8,'tensor'=4] {'dp'}, dimensions={0}, use_global_device_ids=true | all-gather | bytes 589824 | tf_op jit(solution)/shard_map/all_gather | solution.py:149
  33.2 18.2 %all_gather.34 = bf16[2048,128]{1,0:T(8,128)(2,1)} all-gather(bf16[256,128]{1,0:T(8,128)(2,1)S(1)} %copy-done.33), channel_id=1, replica_groups=mesh['dp'=8,'tensor'=4] {'dp'}, dimensions={0}, use_global_device_ids=true | all-gather | bytes 589824 | tf_op jit(solution)/shard_map/all_gather | solution.py:150
  51.5 50.4 %all-gather.10.cloned.1.call-done = bf16[1024,2048]{1,0:T(8,128)(2,1)} async-done(((bf16[256,2048]{1,0:T(8,128)(2,1)}), bf16[1024,2048]{1,0:T(8,128)(2,1)}) %all-gather.10.cloned.1.call-update) | async-done | bytes 4194320 | tf_op jit(solution)/shard_map/all_gather | solution.py:164
  101.8 6.6 fusion.74
  108.4 3.0 reshape.367
  117.2 3.5 convolution_convert_fusion.8
  121.3 14.8 %while.26 = (s32[]{:T(128)}, bf16[2,512,512]{2,1,0:T(8,128)(2,1)}, f32[2,2,4,512,1]{3,2,1,4,0:T(4,128)S(1)}, bf16[2,512,2,64]{1,3,2,0:T(8,128)(2,1)S(1)}, s32[2,...) while((s32[]{:T(128)}, bf16[2,512,512]{2,1,0:T(8,128)(2,1)}, ...), condition=%wide.region_4.5_spmd, body=%wide.region_1.4_spmd.sunk | while | flops 564130816 | bytes 32913000 | solution.py:184
  125.1 2.6 fusion.157
  132.4 2.6 fusion.157
  136.2 6.4 convolution_convert_fusion.3
  143.3 52.2 %reduce-scatter.12.cloned.1.call-done = bf16[256,2048]{1,0:T(8,128)(2,1)} async-done(((bf16[1024,2048]{1,0:T(8,128)(2,1)}), bf16[256,2048]{1,0:T(8,128)(2,1)}) %reduce-scatter.12.cloned.1.call-update) | async-done | bytes 1048592 | tf_op jit(solution)/shard_map/reduce_scatter | solution.py:128
  197.1 2.6 multiply_convert_fusion.5
  202.0 76.9 %all-gather.18.cloned.1.call-done = bf16[2048,2048]{1,0:T(8,128)(2,1)} async-done(((bf16[256,2048]{1,0:T(8,128)(2,1)}), bf16[2048,2048]{1,0:T(8,128)(2,1)}) %all-gather.18.cloned.1.call-update) | async-done | bytes 8388624 | tf_op jit(solution)/shard_map/all_gather | solution.py:152
  279.0 53.4 %all-gather.16.cloned.1.call-done = bf16[1024,2048]{1,0:T(8,128)(2,1)} async-done(((bf16[256,2048]{1,0:T(8,128)(2,1)}), bf16[1024,2048]{1,0:T(8,128)(2,1)}) %all-gather.16.cloned.1.call-update) | async-done | bytes 4194320 | tf_op jit(solution)/shard_map/all_gather | solution.py:188
  332.3 14.6 %fusion.75 = f32[1024,2048]{1,0:T(8,128)} fusion(bf16[1024,2048]{1,0:T(8,128)(2,1)} %all-gather.16.cloned.1.call-done, bf16[2048,2048]{1,0:T(8,128)(2,1)} %all-gather.18.cloned.1.call-done), kind=kOutput, calls=%fused_computation.143 | convolution fusion | flops 8589934592 | bytes 20971520 | tf_op jit(solution)/shard_map/dot_general | solution.py:194
  347.0 69.0 %all-gather.20.cloned.1.call-done = bf16[2048,2048]{1,0:T(8,128)(2,1)} async-done(((bf16[256,2048]{1,0:T(8,128)(2,1)}), bf16[2048,2048]{1,0:T(8,128)(2,1)}) %all-gather.20.cloned.1.call-update) | async-done | bytes 8388624 | tf_op jit(solution)/shard_map/all_gather | solution.py:153
  416.0 14.5 %fusion.76 = f32[1024,2048]{1,0:T(8,128)} fusion(bf16[1024,2048]{1,0:T(8,128)(2,1)} %all-gather.16.cloned.1.call-done, bf16[2048,2048]{1,0:T(8,128)(2,1)} %all-gather.20.cloned.1.call-done), kind=kOutput, calls=%fused_computation.144 | convolution fusion | flops 8589934592 | bytes 20971520 | tf_op jit(solution)/shard_map/dot_general | solution.py:195
  430.5 38.5 %all-gather.24.cloned.1.call-done = bf16[1024,2048]{1,0:T(8,128)(2,1)} async-done(((bf16[256,2048]{1,0:T(8,128)(2,1)}), bf16[1024,2048]{1,0:T(8,128)(2,1)}) %all-gather.24.cloned.1.call-update) | async-done | bytes 4194320 | tf_op jit(solution)/shard_map/all_gather | solution.py:202
  468.9 83.7 %all-gather.22.cloned.1.call-done = bf16[2048,2048]{1,0:T(8,128)(2,1)} async-done(((bf16[256,2048]{1,0:T(8,128)(2,1)}), bf16[2048,2048]{1,0:T(8,128)(2,1)}) %all-gather.22.cloned.1.call-update) | async-done | bytes 8388624 | tf_op jit(solution)/shard_map/all_gather | solution.py:154
  552.6 21.1 %multiply_convert_fusion.1 = (bf16[1024,2048]{1,0:T(8,128)(2,1)S(1)}, bf16[1024,2048]{1,0:T(8,128)(2,1)}, bf16[1024,2048]{1,0:T(8,128)(2,1)}) fusion(f32[1024,2048]{1,0:T(8,128)} %fusion.75, f32[1024,2048]{1,0:T(8,128)} %fusion.76, bf16[1024,2048]{1,0:T(8,128)(2,1)} %all-gather.24.cloned.1.call-done, bf16[2048,2048]{1,0:T(8,128)(2,1)} %all-gather.22.cloned.1.call-done), kind=kOutput, calls=%fused_computation.64 | convolution fusion | flops 8621391872 | bytes 41943040 | tf_op jit(solution)/shard_map/dot_general | solution.py:203
  573.7 16.6 %fusion.77 = f32[1024,2048]{1,0:T(8,128)} fusion(bf16[1024,2048]{1,0:T(8,128)(2,1)} %get-tuple-element.211, bf16[2048,2048]{1,0:T(8,128)(2,1)} %all-gather.18.cloned.1.call-done), kind=kOutput, calls=%fused_computation.145 | convolution fusion | flops 8589934592 | bytes 20971520 | tf_op jit(solution)/shard_map/dot_general | solution.py:67
  590.4 12.4 add_convert_fusion.1
  602.8 51.2 %reduce-scatter.16.cloned.1.call-done = bf16[256,2048]{1,0:T(8,128)(2,1)} async-done(((bf16[1024,2048]{1,0:T(8,128)(2,1)}), bf16[256,2048]{1,0:T(8,128)(2,1)}) %reduce-scatter.16.cloned.1.call-update) | async-done | bytes 1048592 | tf_op jit(solution)/shard_map/reduce_scatter | solution.py:128
  654.0 2.5 fusion.53
  656.6 3.4 fusion.69
  660.0 52.6 %all-gather.26.cloned.1.call-done = bf16[1024,2048]{1,0:T(8,128)(2,1)} async-done(((bf16[256,2048]{1,0:T(8,128)(2,1)}), bf16[1024,2048]{1,0:T(8,128)(2,1)}) %all-gather.26.cloned.1.call-update) | async-done | bytes 4194320 | tf_op jit(solution)/shard_map/all_gather | solution.py:218
  712.7 5.2 multiply_convert_fusion.4
  717.9 105.9 %while.27 = (s32[]{:T(128)}, f32[2,512,8,64]{1,0,3,2:T(2,128)}, f32[2,512,2,64]{1,0,3,2:T(2,128)}, bf16[2,512,2,64]{1,3,2,0:T(8,128)(2,1)}, bf16[2,512,2,64]{1,3...) while((s32[]{:T(128)}, f32[2,512,8,64]{1,0,3,2:T(2,128)}, ...), condition=%wide.region_12.13_spmd, body=%wide.region_10.12_spmd.sunk | while | flops 1365045760 | bytes 147417520 | solution.py:226
  718.4 2.4 fusion.167
  721.2 5.4 fusion.169
  726.6 8.1 fusion.170
  738.6 19.7 %dynamic_update_slice.30 = f32[2,512,8,64]{1,0,3,2:T(2,128)} dynamic-update-slice(f32[2,512,8,64]{1,0,3,2:T(2,128)} %get-tuple-element.382, f32[1,512,8,64]{1,0,3,2:T(1,128)S(1)} %copy.94, s32[]{:T(128)} %get-tuple-element.381, s32[]{:T(128)} %constant.45.clone.1..sunk, s32[]{:T(128)} %constant.45.clone.1..sunk, s32[]{:T(128)} %constant.45.clone.1..sunk) | dynamic-update-slice | bytes 2097156 | tf_op jit(solution)/shard_map/while/body/jit(dynamic_update_index_in_dim)/dynamic_update_slice | solution.py:226
  758.2 3.6 fusion.171
  762.1 2.4 dynamic_update_slice.31
  765.4 5.6 fusion.172
  771.2 2.4 fusion.167
  774.0 5.4 fusion.169
  779.4 8.1 fusion.170
  791.4 19.7 %dynamic_update_slice.30 = f32[2,512,8,64]{1,0,3,2:T(2,128)} dynamic-update-slice(f32[2,512,8,64]{1,0,3,2:T(2,128)} %get-tuple-element.382, f32[1,512,8,64]{1,0,3,2:T(1,128)S(1)} %copy.94, s32[]{:T(128)} %get-tuple-element.381, s32[]{:T(128)} %constant.45.clone.1..sunk, s32[]{:T(128)} %constant.45.clone.1..sunk, s32[]{:T(128)} %constant.45.clone.1..sunk) | dynamic-update-slice | bytes 2097156 | tf_op jit(solution)/shard_map/while/body/jit(dynamic_update_index_in_dim)/dynamic_update_slice | solution.py:226
  811.1 3.6 fusion.171
  814.9 2.4 dynamic_update_slice.31
  818.2 5.6 fusion.172
  829.8 4.3 convolution_convert_fusion.6
  834.1 14.1 %convolution_convert_fusion.1 = bf16[2048,2048]{1,0:T(8,128)(2,1)} fusion(bf16[1024,2048]{1,0:T(8,128)(2,1)} %all-gather.16.cloned.1.call-done, bf16[1024,2048]{1,0:T(8,128)(2,1)} %get-tuple-element.211), kind=kOutput, calls=%fused_computation.70 | convolution fusion | flops 8594128896 | bytes 16777216 | tf_op jit(solution)/shard_map/dot_general | solution.py:61
  848.3 14.2 %convolution_convert_fusion = bf16[2048,2048]{1,0:T(8,128)(2,1)} fusion(bf16[1024,2048]{1,0:T(8,128)(2,1)} %all-gather.16.cloned.1.call-done, bf16[1024,2048]{1,0:T(8,128)(2,1)} %copy-done.48), kind=kOutput, calls=%fused_computation.69 | convolution fusion | flops 8594128896 | bytes 16777216 | tf_op jit(solution)/shard_map/dot_general | solution.py:61
  863.0 14.0 %convert_bitcast_fusion = bf16[2048,2048]{0,1:T(8,128)(2,1)} fusion(bf16[1024,2048]{1,0:T(8,128)(2,1)} %get-tuple-element.212, bf16[1024,2048]{1,0:T(8,128)(2,1)} %all-gather.24.cloned.1.call-done), kind=kOutput, calls=%fused_computation.61 | convolution fusion | flops 8594128896 | bytes 16777216 | tf_op jit(solution)/shard_map/dot_general | solution.py:61
  877.1 6.3 convolution_convert_fusion.4
  887.4 3.8 convolution_convert_fusion.5
  893.1 2.4 fusion.78
  895.5 3.4 add_convert_fusion
  898.9 14.3 %convolution_convert_fusion.2 = bf16[1024,2048]{1,0:T(8,128)(2,1)} fusion(bf16[1024,2048]{1,0:T(8,128)(2,1)} %get-tuple-element.212, bf16[2048,2048]{1,0:T(8,128)(2,1)} %all-gather.22.cloned.1.call-done), kind=kOutput, calls=%fused_computation.77 | convolution fusion | flops 8592031744 | bytes 16777216 | tf_op jit(solution)/shard_map/dot_general | solution.py:67
  916.3 66.6 %reduce-scatter.28.cloned.1.call-done = bf16[256,2048]{1,0:T(8,128)(2,1)} async-done(((bf16[2048,2048]{1,0:T(8,128)(2,1)}), bf16[256,2048]{1,0:T(8,128)(2,1)}) %reduce-scatter.28.cloned.1.call-update) | async-done | bytes 1048592 | tf_op jit(solution)/shard_map/reduce_scatter | solution.py:128
  982.9 2.8 convert_element_type.184
  985.7 87.4 %reduce-scatter.30.cloned.1.call-done = bf16[256,2048]{1,0:T(8,128)(2,1)} async-done(((bf16[2048,2048]{1,0:T(8,128)(2,1)}), bf16[256,2048]{1,0:T(8,128)(2,1)}) %reduce-scatter.30.cloned.1.call-update) | async-done | bytes 1048592 | tf_op jit(solution)/shard_map/reduce_scatter | solution.py:128
  1073.0 2.8 convert_element_type.186
  1075.9 87.3 %reduce-scatter.32.cloned.1.call-done = bf16[256,2048]{0,1:T(8,128)(2,1)} async-done(((bf16[2048,2048]{0,1:T(8,128)(2,1)}), bf16[256,2048]{0,1:T(8,128)(2,1)}) %reduce-scatter.32.cloned.1.call-update) | async-done | bytes 1048592 | tf_op jit(solution)/shard_map/reduce_scatter | solution.py:128
  1163.2 2.6 copy.57
  1165.8 34.1 %reduce-scatter.26.cloned.1.call-done = bf16[256,512]{1,0:T(8,128)(2,1)} async-done(((bf16[2048,512]{1,0:T(8,128)(2,1)}), bf16[256,512]{1,0:T(8,128)(2,1)}) %reduce-scatter.26.cloned.1.call-update) | async-done | bytes 262160 | tf_op jit(solution)/shard_map/reduce_scatter | solution.py:128
  1201.7 35.0 %reduce-scatter.20.cloned.1.call-done = bf16[256,512]{1,0:T(8,128)(2,1)} async-done(((bf16[2048,512]{1,0:T(8,128)(2,1)}), bf16[256,512]{1,0:T(8,128)(2,1)}) %reduce-scatter.20.cloned.1.call-update) | async-done | bytes 262160 | tf_op jit(solution)/shard_map/reduce_scatter | solution.py:128
  1238.5 52.4 %reduce-scatter.18.cloned.1.call-done = bf16[256,2048]{1,0:T(8,128)(2,1)} async-done(((bf16[1024,2048]{1,0:T(8,128)(2,1)}), bf16[256,2048]{1,0:T(8,128)(2,1)}) %reduce-scatter.18.cloned.1.call-update) | async-done | bytes 1048592 | tf_op jit(solution)/shard_map/reduce_scatter | solution.py:128
  1292.8 39.9 %all-reduce = (f32[2048]{0:T(1024)}, f32[2048]{0:T(1024)}) all-reduce(f32[2048]{0:T(1024)S(1)} %get-tuple-element.166, f32[2048]{0:T(1024)S(1)} %copy-done.34), channel_id=1, replica_groups=mesh['dp'=8,'tensor'=4] {'dp','tensor'}, use_global_device_ids=true, to_apply=%region_23.24 | all-reduce | flops 4096 | bytes 32768 | tf_op jit(solution)/shard_map/psum | solution.py:262
  1332.7 14.0 %reduce-scatter.14.cloned.1.call-done = bf16[256,2048]{1,0:T(8,128)(2,1)} async-done(((bf16[1024,2048]{1,0:T(8,128)(2,1)}), bf16[256,2048]{1,0:T(8,128)(2,1)}) %reduce-scatter.14.cloned.1.call-update) | async-done | bytes 1048592 | tf_op jit(solution)/shard_map/reduce_scatter | solution.py:128
  1346.7 4.4 fusion.48
  (243 shorter events, 57.1 us)
Async XLA Ops:
  7.2 7.2 copy-start.32
  7.2 26.0 %copy-start.33 = (bf16[256,128]{1,0:T(8,128)(2,1)S(1)}, bf16[256,128]{1,0:T(8,128)(2,1)}, u32[]{:S(2)}) copy-start(bf16[256,128]{1,0:T(8,128)(2,1)} %param.20) | copy-start | bytes 196612
  7.2 44.2 %copy-start.39 = (s32[1024]{0:T(1024)S(1)}, s32[1024]{0:T(1024)}, u32[]{:S(2)}) copy-start(s32[1024]{0:T(1024)} %param.26) | copy-start | bytes 12292
  7.2 44.2 %all-gather.12.cloned.1.call-start = ((), (), s32[]{:S(2)}) async-start(), calls=%async_computation.12 | async-start | bytes 2359296 | tf_op jit(solution)/shard_map/all_gather | solution.py:148
  7.9 93.9 %all-gather.10.cloned.1.call-start = ((), (), s32[]{:S(2)}) async-start(), calls=%async_computation.11 | async-start | bytes 5242880 | tf_op jit(solution)/shard_map/all_gather | solution.py:164
  13.2 123.0 %all-gather.14.cloned.1.call-start = ((), (), s32[]{:S(2)}) async-start(), calls=%async_computation.13 | async-start | bytes 2359296 | tf_op jit(solution)/shard_map/all_gather | solution.py:151
  13.9 181.5 %reduce-scatter.12.cloned.1.call-start = ((), (), s32[]{:S(2)}) async-start(), calls=%async_computation.14 | async-start | bytes 5242880 | tf_op jit(solution)/shard_map/reduce_scatter | solution.py:128
  14.3 102.3 %copy-start.17 = (f32[512,64]{0,1:T(8,128)}, f32[512,64]{0,1:T(8,128)S(1)}, u32[]{:S(2)}) copy-start(f32[512,64]{0,1:T(8,128)S(1)} %get-tuple-element.224) | copy-start | bytes 393220
  14.4 102.3 %copy-start.19 = (f32[512,64]{0,1:T(8,128)}, f32[512,64]{0,1:T(8,128)S(1)}, u32[]{:S(2)}) copy-start(f32[512,64]{0,1:T(8,128)S(1)} %get-tuple-element.223) | copy-start | bytes 393220
  33.2 80.8 %copy-start.12 = (bf16[2048,128]{1,0:T(8,128)(2,1)}, bf16[2048,128]{1,0:T(8,128)(2,1)S(1)}, u32[]{:S(2)}) copy-start(bf16[2048,128]{1,0:T(8,128)(2,1)S(1)} %all_gather.35) | copy-start | bytes 1572868
  136.2 6.4 copy-start.21
  136.2 6.4 copy-start.27
  142.6 52.9 %copy-start.2 = (bf16[256,2048]{1,0:T(8,128)(2,1)S(1)}, bf16[256,2048]{1,0:T(8,128)(2,1)}, u32[]{:S(2)}) copy-start(bf16[256,2048]{1,0:T(8,128)(2,1)} %param.16) | copy-start | bytes 3145732
  142.6 54.6 %copy-start.29 = (f32[2048]{0:T(1024)S(1)}, f32[2048]{0:T(1024)}, u32[]{:S(2)}) copy-start(f32[2048]{0:T(1024)} %param.22) | copy-start | bytes 24580
  142.6 136.4 %all-gather.18.cloned.1.call-start = ((), (), s32[]{:S(2)}) async-start(), calls=%async_computation.16 | async-start | bytes 9437184 | tf_op jit(solution)/shard_map/all_gather | solution.py:152
  143.2 189.1 %all-gather.16.cloned.1.call-start = ((), (), s32[]{:S(2)}) async-start(), calls=%async_computation.15 | async-start | bytes 5242880 | tf_op jit(solution)/shard_map/all_gather | solution.py:188
  197.1 459.4 %copy-start.35 = (f32[256]{0:T(256)}, f32[256]{0:T(256)S(1)}, u32[]{:S(2)}) copy-start(f32[256]{0:T(256)S(1)} %get-tuple-element.228) | copy-start | bytes 3076
  197.1 459.4 %copy-start.41 = (f32[256]{0:T(256)}, f32[256]{0:T(256)S(1)}, u32[]{:S(2)}) copy-start(f32[256]{0:T(256)S(1)} %get-tuple-element.227) | copy-start | bytes 3076
  199.8 216.3 %all-gather.20.cloned.1.call-start = ((), (), s32[]{:S(2)}) async-start(), calls=%async_computation.17 | async-start | bytes 9437184 | tf_op jit(solution)/shard_map/all_gather | solution.py:153
  200.5 268.4 %all-gather.24.cloned.1.call-start = ((), (), s32[]{:S(2)}) async-start(), calls=%async_computation.20 | async-start | bytes 5242880 | tf_op jit(solution)/shard_map/all_gather | solution.py:202
  201.3 351.4 %all-gather.22.cloned.1.call-start = ((), (), s32[]{:S(2)}) async-start(), calls=%async_computation.18 | async-start | bytes 9437184 | tf_op jit(solution)/shard_map/all_gather | solution.py:154
  202.0 452.0 %reduce-scatter.16.cloned.1.call-start = ((), (), s32[]{:S(2)}) async-start(), calls=%async_computation.21 | async-start | bytes 5242880 | tf_op jit(solution)/shard_map/reduce_scatter | solution.py:128
  573.7 16.6 %copy-start.48 = (bf16[1024,2048]{1,0:T(8,128)(2,1)}, bf16[1024,2048]{1,0:T(8,128)(2,1)S(1)}, u32[]{:S(2)}) copy-start(bf16[1024,2048]{1,0:T(8,128)(2,1)S(1)} %get-tuple-element.210) | copy-start | bytes 12582916
  573.7 16.6 %copy-start.46 = (bf16[2048,2048]{1,0:T(8,128)(2,1)S(1)}, bf16[2048,2048]{1,0:T(8,128)(2,1)}, u32[]{:S(2)}) copy-start(bf16[2048,2048]{1,0:T(8,128)(2,1)} %all-gather.20.cloned.1.call-done) | copy-start | bytes 25165828
  602.7 51.3 %copy-start.6 = (bf16[256,2048]{1,0:T(8,128)(2,1)S(1)}, bf16[256,2048]{1,0:T(8,128)(2,1)}, u32[]{:S(2)}) copy-start(bf16[256,2048]{1,0:T(8,128)(2,1)} %reduce-scatter.12.cloned.1.call-done) | copy-start | bytes 3145732
  602.8 57.3 %copy-start.40 = (s32[1024]{0:T(1024)S(1)}, s32[1024]{0:T(1024)}, u32[]{:S(2)}) copy-start(s32[1024]{0:T(1024)} %param.26) | copy-start | bytes 12292
  602.8 109.9 %all-gather.26.cloned.1.call-start = ((), (), s32[]{:S(2)}) async-start(), calls=%async_computation.22 | async-start | bytes 5242880 | tf_op jit(solution)/shard_map/all_gather | solution.py:218
  656.6 61.3 %copy-start.43 = (f32[256]{0:T(256)}, f32[256]{0:T(256)S(1)}, u32[]{:S(2)}) copy-start(f32[256]{0:T(256)S(1)} %broadcast_multiply_fusion.3) | copy-start | bytes 3076
  659.9 253.4 %reduce-scatter.22.cloned.1.call-start = ((), (), s32[]{:S(2)}) async-start(), calls=%async_computation.25 | async-start | bytes 589824 | tf_op jit(solution)/shard_map/reduce_scatter | solution.py:128
  717.9 105.9 %copy-start.18 = (f32[512,64]{0,1:T(8,128)S(1)}, f32[512,64]{0,1:T(8,128)}, u32[]{:S(2)}) copy-start(f32[512,64]{0,1:T(8,128)} %copy-done.17) | copy-start | bytes 393220
  718.1 3.0 copy-start.4
  718.4 2.8 copy-start.28
  720.8 5.8 copy-start.1
  738.6 23.5 %copy-start.24 = (f32[2,512,2,64]{1,0,3,2:T(2,128)S(1)}, f32[2,512,2,64]{1,0,3,2:T(2,128)}, u32[]{:S(2)}) copy-start(f32[2,512,2,64]{1,0,3,2:T(2,128)} %get-tuple-element.383) | copy-start | bytes 1572868 | tf_op jit(solution)/shard_map/while
  765.3 5.6 copy-start.5
  765.4 5.6 copy-start.11
  770.9 3.0 copy-start.4
  773.6 5.8 copy-start.1
  791.4 23.5 %copy-start.24 = (f32[2,512,2,64]{1,0,3,2:T(2,128)S(1)}, f32[2,512,2,64]{1,0,3,2:T(2,128)}, u32[]{:S(2)}) copy-start(f32[2,512,2,64]{1,0,3,2:T(2,128)} %get-tuple-element.383) | copy-start | bytes 1572868 | tf_op jit(solution)/shard_map/while
  818.2 5.6 copy-start.5
  818.2 5.6 copy-start.11
  823.8 3.2 copy-start.15
  825.5 4.0 copy-start.26
  829.2 85.6 %reduce-scatter.24.cloned.1.call-start = ((), (), s32[]{:S(2)}) async-start(), calls=%async_computation.26 | async-start | bytes 589824 | tf_op jit(solution)/shard_map/reduce_scatter | solution.py:128
  834.1 148.8 %reduce-scatter.28.cloned.1.call-start = ((), (), s32[]{:S(2)}) async-start(), calls=%async_computation.28 | async-start | bytes 9437184 | tf_op jit(solution)/shard_map/reduce_scatter | solution.py:128
  848.3 224.8 %reduce-scatter.30.cloned.1.call-start = ((), (), s32[]{:S(2)}) async-start(), calls=%async_computation.29 | async-start | bytes 9437184 | tf_op jit(solution)/shard_map/reduce_scatter | solution.py:128
  862.5 300.7 %reduce-scatter.32.cloned.1.call-start = ((), (), s32[]{:S(2)}) async-start(), calls=%async_computation.30 | async-start | bytes 9437184 | tf_op jit(solution)/shard_map/reduce_scatter | solution.py:128
  877.0 6.5 copy-start.9
  877.1 322.8 %reduce-scatter.26.cloned.1.call-start = ((), (), s32[]{:S(2)}) async-start(), calls=%async_computation.27 | async-start | bytes 2359296 | tf_op jit(solution)/shard_map/reduce_scatter | solution.py:128
  883.4 353.3 %reduce-scatter.20.cloned.1.call-start = ((), (), s32[]{:S(2)}) async-start(), calls=%async_computation.24 | async-start | bytes 2359296 | tf_op jit(solution)/shard_map/reduce_scatter | solution.py:128
  887.4 4.1 copy-start.13
  891.3 399.7 %reduce-scatter.18.cloned.1.call-start = ((), (), s32[]{:S(2)}) async-start(), calls=%async_computation.23 | async-start | bytes 5242880 | tf_op jit(solution)/shard_map/reduce_scatter | solution.py:128
  898.9 447.7 %reduce-scatter.14.cloned.1.call-start = ((), (), s32[]{:S(2)}) async-start(), calls=%async_computation.19 | async-start | bytes 5242880 | tf_op jit(solution)/shard_map/reduce_scatter | solution.py:128
  985.7 305.3 %copy-start.3 = (bf16[256,2048]{1,0:T(8,128)(2,1)S(1)}, bf16[256,2048]{1,0:T(8,128)(2,1)}, u32[]{:S(2)}) copy-start(bf16[256,2048]{1,0:T(8,128)(2,1)} %param.16) | copy-start | bytes 3145732
  985.7 305.3 %copy-start.31 = (f32[2048]{0:T(1024)S(1)}, f32[2048]{0:T(1024)}, u32[]{:S(2)}) copy-start(f32[2048]{0:T(1024)} %param.17) | copy-start | bytes 24580
  985.7 305.3 %copy-start.38 = (f32[256]{0:T(256)S(1)}, f32[256]{0:T(256)}, u32[]{:S(2)}) copy-start(f32[256]{0:T(256)} %copy-done.37) | copy-start | bytes 3076
  1075.8 217.0 %copy-start.34 = (f32[2048]{0:T(1024)S(1)}, f32[2048]{0:T(1024)}, u32[]{:S(2)}) copy-start(f32[2048]{0:T(1024)} %get-tuple-element.164) | copy-start | bytes 24580
  1075.8 270.8 %copy-start.7 = (bf16[256,2048]{1,0:T(8,128)(2,1)S(1)}, bf16[256,2048]{1,0:T(8,128)(2,1)}, u32[]{:S(2)}) copy-start(bf16[256,2048]{1,0:T(8,128)(2,1)} %reduce-scatter.12.cloned.1.call-done) | copy-start | bytes 3145732
  1075.8 270.8 %copy-start.8 = (bf16[256,2048]{1,0:T(8,128)(2,1)S(1)}, bf16[256,2048]{1,0:T(8,128)(2,1)}, u32[]{:S(2)}) copy-start(bf16[256,2048]{1,0:T(8,128)(2,1)} %param.27) | copy-start | bytes 3145732
  1075.8 270.8 %copy-start.30 = (f32[2048]{0:T(1024)S(1)}, f32[2048]{0:T(1024)}, u32[]{:S(2)}) copy-start(f32[2048]{0:T(1024)} %param.22) | copy-start | bytes 24580
  1075.8 270.8 %copy-start.36 = (f32[256]{0:T(256)S(1)}, f32[256]{0:T(256)}, u32[]{:S(2)}) copy-start(f32[256]{0:T(256)} %copy-done.35) | copy-start | bytes 3076
  1075.8 270.8 %copy-start.42 = (f32[256]{0:T(256)S(1)}, f32[256]{0:T(256)}, u32[]{:S(2)}) copy-start(f32[256]{0:T(256)} %copy-done.41) | copy-start | bytes 3076
  1075.9 270.8 %copy-start.44 = (f32[256]{0:T(256)S(1)}, f32[256]{0:T(256)}, u32[]{:S(2)}) copy-start(f32[256]{0:T(256)} %copy-done.43) | copy-start | bytes 3076
  1075.9 270.8 %copy-start.45 = (f32[256]{0:T(256)S(1)}, f32[256]{0:T(256)}, u32[]{:S(2)}) copy-start(f32[256]{0:T(256)} %get-tuple-element.225) | copy-start | bytes 3076
  (14 other events, 27.1 us)
Sparse Core Ops, SparseCore 0:
  9.6 37.0 all-gather.11
  49.1 52.6 all-gather.9
  103.5 29.1 all-gather.13
  142.7 52.6 reduce-scatter.11
  196.9 82.0 all-gather.17
  281.3 51.0 all-gather.15
  333.9 82.0 all-gather.19
  417.9 51.0 all-gather.23
  470.6 82.0 all-gather.21
  602.9 51.0 reduce-scatter.15
  660.1 52.5 all-gather.25
  829.3 31.2 reduce-scatter.21
  863.5 29.4 reduce-scatter.23
  895.1 87.7 reduce-scatter.27
  985.0 87.9 reduce-scatter.29
  1075.2 87.9 reduce-scatter.31
  1165.3 34.5 reduce-scatter.25
  1202.0 34.6 reduce-scatter.19
  1239.7 51.1 reduce-scatter.17
  1293.7 52.8 reduce-scatter.13
where the time goes:
time: 1370 us; the launch traced here: 1360 us
  waiting for transfers between devices  909 us (66%)
  matrix products  226 us (16%)
  blocking collectives  76.9 us (6%)
  local copies, waits for them, and re-layouts  64.8 us (5%)
  other arithmetic  63.8 us (5%)
  between operations  15.1 us (1%)
    reduce_scatter x11, waiting for transfers between devices, sum_rows(): lax.psum_scatter(partial.astype(jnp.bfloat16), axis, scatter_dimension=0,...  480 us
    all_gather x1, waiting for transfers between devices, per_device(): lax.all_gather(w_down, 'dp', axis=0, tiled=True)  83.7 us
    all_gather x1, waiting for transfers between devices, per_device(): lax.all_gather(w_gate, 'dp', axis=0, tiled=True)  76.9 us
    all_gather x1, waiting for transfers between devices, per_device(): lax.all_gather(w_up, 'dp', axis=0, tiled=True)  69 us
    dot_general x7, matrix products, contract_rows(): lax.dot_general(left_side, right_side, (((0,), (0,)), ((), ())), preferre...  58.9 us
    dot_general x7, matrix products, contract_cols(): lax.dot_general(left_side, right_side, (((1,), (1,)), ((), ())), preferre...  56.7 us
    all_gather x1, waiting for transfers between devices, per_device(): lax.all_gather((residual_own * scale_two_own * mlp_gain[None, :]).astype(...  53.4 us
    all_gather x1, waiting for transfers between devices, per_device(): lax.all_gather(grad_residual_own.astype(jnp.bfloat16), 'tensor', axis=0,...  52.6 us
  transfers between devices with their start and end apart: 20, of which 16 were waited for; matrix products, arithmetic and copies ran while one was open for 13% of the time, Pallas kernels for 0%

commit v1 on v0

--- a/solution.py
+++ b/solution.py
@@ -8,6 +8,40 @@
 EPSILON = 1e-05
 ROPE_BASE = 500000.0
 NEG_LARGE = -1e30
+
+
+def _launch_paths(unit, named_axis, d_out):
+    value_now = lax.axis_size(named_axis)
+    high, later, piece_out = (value_now, lax.axis_index(named_axis), unit.shape[d_out])
+    table = []
+    j0 = 0
+    while j0 < high:
+        table.append((j0, (j0 + 1) % high))
+        j0 = j0 + 1
+    seen = []
+    j0 = 0
+    while j0 < high:
+        seen.append((j0, (j0 - 1) % high))
+        j0 = j0 + 1
+    m_next = jnp.zeros(
+        (*unit.shape[:d_out], high * piece_out, *unit.shape[d_out + 1 :]), unit.dtype
+    )
+    m_next = lax.dynamic_update_slice_in_dim(m_next, unit, later * piece_out, axis=d_out)
+    long_array = placed = unit
+    u1 = high // 2
+    dev = 1
+    while dev < u1 + 1:
+        long_array = lax.ppermute(long_array, perm=table, axis_name=named_axis)
+        m_next = lax.dynamic_update_slice_in_dim(
+            m_next, long_array, (later - dev) % high * piece_out, axis=d_out
+        )
+        if dev < high - u1:
+            placed = lax.ppermute(placed, axis_name=named_axis, perm=seen)
+            m_next = lax.dynamic_update_slice_in_dim(
+                m_next, placed, (later + dev) % high * piece_out, axis=d_out
+            )
+        dev = dev + 1
+    return m_next
 
 
 def rotary_tables(length, head_dim):
@@ -149,7 +183,7 @@
         lax.all_gather(w_key, "dp", axis=0, tiled=True),
         lax.all_gather(w_value, "dp", axis=0, tiled=True),
         lax.all_gather(w_out, "dp", axis=0, tiled=True),
-        lax.all_gather(w_gate, "dp", axis=0, tiled=True),
+        _launch_paths(w_gate, "dp", 0),
         lax.all_gather(w_up, "dp", axis=0, tiled=True),
         lax.all_gather(w_down, "dp", axis=0, tiled=True),
     )

time: 1370 us -> 1310 us (0.956)
  waiting for transfers between devices: 909 us -> 823 us
  local copies, waits for them, and re-layouts: 64.8 us -> 86.1 us
    all_gather x1 -> x0, waiting for transfers between devices: 76.9 us -> none  [per_device(): lax.all_gather(w_gate, 'dp', axis=0, tiled=True)]
    ppermute x0 -> x7, waiting for transfers between devices: none -> 64.1 us  [the longest x3 64.1 us: _launch_paths(): placed = lax.ppermute(placed, axis_name=named_axis, perm=seen)]
    all_gather x1, waiting for transfers between devices: 38.5 us -> 0.01 us  [per_device(): grad_full = lax.all_gather(cotangent, 'tensor', axis=0, tiled=True)]
    all_gather x1, waiting for transfers between devices: 83.7 us -> 49.5 us  [per_device(): lax.all_gather(w_down, 'dp', axis=0, tiled=True)]
    dynamic_update_slice x0 -> x8, local copies, waits for them, and re-layouts: none -> 14.8 us  [the longest x4 8.09 us: _launch_paths(): lax.dynamic_update_slice_in_dim(m_next, long_array, (later - dev) % high...]
  transfers between devices with their start and end apart: 20 -> 26, of which waited for: 16 -> 17; matrix products, arithmetic and copies ran while one was open for 13% -> 14% of each run, Pallas kernels for 0% -> 0%
where the time goes in v1:
time: 1310 us; the launch traced here: 1300 us
  waiting for transfers between devices  823 us (63%)
  matrix products  222 us (17%)
  local copies, waits for them, and re-layouts  86.1 us (7%)
  blocking collectives  76.9 us (6%)
  other arithmetic  64.5 us (5%)
  between operations  14.8 us (1%)
    reduce_scatter x11, waiting for transfers between devices, sum_rows(): lax.psum_scatter(partial.astype(jnp.bfloat16), axis, scatter_dimension=0,...  481 us
    all_gather x1, waiting for transfers between devices, per_device(): lax.all_gather(w_up, 'dp', axis=0, tiled=True)  69.5 us
    ppermute x3, waiting for transfers between devices, _launch_paths(): placed = lax.ppermute(placed, axis_name=named_axis, perm=seen)  64.1 us
    dot_general x7, matrix products, contract_rows(): lax.dot_general(left_side, right_side, (((0,), (0,)), ((), ())), preferre...  58.8 us
    all_gather x1, waiting for transfers between devices, per_device(): lax.all_gather((residual_own * scale_two_own * mlp_gain[None, :]).astype(...  53.5 us
    dot_general x7, matrix products, contract_cols(): lax.dot_general(left_side, right_side, (((1,), (1,)), ((), ())), preferre...  53.5 us
    all_gather x1, waiting for transfers between devices, per_device(): lax.all_gather(grad_residual_own.astype(jnp.bfloat16), 'tensor', axis=0,...  52.6 us
    all_gather x1, waiting for transfers between devices, per_device(): lax.all_gather((input_own * scale_one * attn_gain[None, :]).astype(jnp.bf...  50.3 us
  transfers between devices with their start and end apart: 26, of which 17 were waited for; matrix products, arithmetic and copies ran while one was open for 14% of the time, Pallas kernels for 0%

profile of v1, /device:TPU:0, one launch (start us, length us, event | category | flops | bytes accessed | tf_op | source)
XLA Modules:
  0.0 1300.5 jit_solution(10064902112232264345)
XLA Ops:
  10.7 2.5 fusion.56
  14.4 18.8 %all_gather.32 = bf16[2048,128]{1,0:T(8,128)(2,1)S(1)} all-gather(bf16[256,128]{1,0:T(8,128)(2,1)S(1)} %copy-done.29), channel_id=1, replica_groups=mesh['dp'=8,'tensor'=4] {'dp'}, dimensions={0}, use_global_device_ids=true | all-gather | bytes 589824 | tf_op jit(solution)/shard_map/all_gather | solution.py:183
  33.2 18.3 %all_gather.31 = bf16[2048,128]{1,0:T(8,128)(2,1)} all-gather(bf16[256,128]{1,0:T(8,128)(2,1)S(1)} %copy-done.30), channel_id=1, replica_groups=mesh['dp'=8,'tensor'=4] {'dp'}, dimensions={0}, use_global_device_ids=true | all-gather | bytes 589824 | tf_op jit(solution)/shard_map/all_gather | solution.py:184
  51.5 50.3 %all-gather.9.cloned.1.call-done = bf16[1024,2048]{1,0:T(8,128)(2,1)} async-done(((bf16[256,2048]{1,0:T(8,128)(2,1)}), bf16[1024,2048]{1,0:T(8,128)(2,1)}) %all-gather.9.cloned.1.call-update) | async-done | bytes 4194320 | tf_op jit(solution)/shard_map/all_gather | solution.py:198
  101.8 6.6 fusion.74
  108.4 3.0 reshape.367
  119.1 3.5 convolution_convert_fusion.8
  123.2 14.8 %while.26 = (s32[]{:T(128)}, bf16[2,512,512]{2,1,0:T(8,128)(2,1)}, f32[2,2,4,512,1]{3,2,1,4,0:T(4,128)S(1)}, bf16[2,512,2,64]{1,3,2,0:T(8,128)(2,1)S(1)}, s32[2,...) while((s32[]{:T(128)}, bf16[2,512,512]{2,1,0:T(8,128)(2,1)}, ...), condition=%wide.region_4.5_spmd, body=%wide.region_1.4_spmd.sunk | while | flops 564130816 | bytes 32913000 | solution.py:218
  126.9 2.6 fusion.157
  134.3 2.6 fusion.157
  138.0 6.3 convolution_convert_fusion.3
  146.4 50.8 %reduce-scatter.12.cloned.1.call-done = bf16[256,2048]{1,0:T(8,128)(2,1)} async-done(((bf16[1024,2048]{1,0:T(8,128)(2,1)}), bf16[256,2048]{1,0:T(8,128)(2,1)}) %reduce-scatter.12.cloned.1.call-update) | async-done | bytes 1048592 | tf_op jit(solution)/shard_map/reduce_scatter | solution.py:162
  198.9 2.6 multiply_convert_fusion.5
  201.5 2.7 collective-permute-start.1
  204.2 22.2 %collective-permute-done.1 = bf16[256,2048]{1,0:T(8,128)(2,1)} collective-permute-done((bf16[256,2048]{1,0:T(8,128)(2,1)}, bf16[256,2048]{1,0:T(8,128)(2,1)}, u32[]{:S(2)}, u32[]{:S(2)}) %collective-permute-start.1) | collective-permute-done | bytes 1048608 | tf_op jit(solution)/shard_map/ppermute | solution.py:39
  226.4 3.8 collective-permute-start.3
  230.2 4.3 broadcast_in_dim.72
  235.5 15.0 %collective-permute-done.3 = bf16[256,2048]{1,0:T(8,128)(2,1)} collective-permute-done((bf16[256,2048]{1,0:T(8,128)(2,1)}, bf16[256,2048]{1,0:T(8,128)(2,1)}, u32[]{:S(2)}, u32[]{:S(2)}) %collective-permute-start.3) | collective-permute-done | bytes 1048608 | tf_op jit(solution)/shard_map/ppermute | solution.py:39
  250.6 3.8 collective-permute-start.5
  266.0 26.9 %collective-permute-done.5 = bf16[256,2048]{1,0:T(8,128)(2,1)S(1)} collective-permute-done((bf16[256,2048]{1,0:T(8,128)(2,1)}, bf16[256,2048]{1,0:T(8,128)(2,1)S(1)}, u32[]{:S(2)}, u32[]{:S(2)}) %collective-permute-start.5) | collective-permute-done | bytes 1048608 | tf_op jit(solution)/shard_map/ppermute | solution.py:39
  295.0 49.5 %all-gather.19.cloned.1.call-done = bf16[2048,2048]{1,0:T(8,128)(2,1)} async-done(((bf16[256,2048]{1,0:T(8,128)(2,1)}), bf16[2048,2048]{1,0:T(8,128)(2,1)}) %all-gather.19.cloned.1.call-update) | async-done | bytes 8388624 | tf_op jit(solution)/shard_map/all_gather | solution.py:188
  344.5 14.7 %fusion.76 = f32[1024,2048]{1,0:T(8,128)} fusion(bf16[1024,2048]{1,0:T(8,128)(2,1)} %all-gather.21.cloned.1.call-done, bf16[2048,2048]{1,0:T(8,128)(2,1)} %all-gather.19.cloned.1.call-done), kind=kOutput, calls=%fused_computation.152 | convolution fusion | flops 8589934592 | bytes 20971520 | tf_op jit(solution)/shard_map/dot_general | solution.py:237
  359.2 69.5 %all-gather.17.cloned.1.call-done = bf16[2048,2048]{1,0:T(8,128)(2,1)} async-done(((bf16[256,2048]{1,0:T(8,128)(2,1)}), bf16[2048,2048]{1,0:T(8,128)(2,1)}) %all-gather.17.cloned.1.call-update) | async-done | bytes 8388624 | tf_op jit(solution)/shard_map/all_gather | solution.py:187
  428.7 53.5 %all-gather.15.cloned.1.call-done = bf16[1024,2048]{1,0:T(8,128)(2,1)} async-done(((bf16[256,2048]{1,0:T(8,128)(2,1)}), bf16[1024,2048]{1,0:T(8,128)(2,1)}) %all-gather.15.cloned.1.call-update) | async-done | bytes 4194320 | tf_op jit(solution)/shard_map/all_gather | solution.py:222
  482.2 15.5 %fusion.75 = f32[1024,2048]{1,0:T(8,128)} fusion(bf16[1024,2048]{1,0:T(8,128)(2,1)} %all-gather.15.cloned.1.call-done, bf16[2048,2048]{1,0:T(8,128)(2,1)} %all-gather.17.cloned.1.call-done), kind=kOutput, calls=%fused_computation.151 | convolution fusion | flops 8589934592 | bytes 20971520 | tf_op jit(solution)/shard_map/dot_general | solution.py:229
  497.8 19.7 %multiply_convert_fusion.2 = (bf16[1024,2048]{1,0:T(8,128)(2,1)}, bf16[1024,2048]{1,0:T(8,128)(2,1)}, bf16[1024,2048]{1,0:T(8,128)(2,1)}) fusion(f32[1024,2048]{1,0:T(8,128)} %fusion.76, f32[1024,2048]{1,0:T(8,128)} %fusion.75, bf16[1024,2048]{1,0:T(8,128)(2,1)S(1)} %copy-done.43, bf16[2048,2048]{1,0:T(8,128)(2,1)} %constant_dynamic-update-slice_fusion.1), kind=kOutput, calls=%fused_computation.65 | convolution fusion | flops 8621391872 | bytes 41943040 | tf_op jit(solution)/shard_map/dot_general | solution.py:228
  517.4 13.2 %fusion.77 = f32[1024,2048]{1,0:T(8,128)S(1)} fusion(bf16[1024,2048]{1,0:T(8,128)(2,1)} %get-tuple-element.211, bf16[2048,2048]{1,0:T(8,128)(2,1)} %all-gather.17.cloned.1.call-done), kind=kOutput, calls=%fused_computation.153 | convolution fusion | flops 8589934592 | bytes 20971520 | tf_op jit(solution)/shard_map/dot_general | solution.py:101
  530.6 12.9 add_convert_fusion.1
  543.6 52.7 %reduce-scatter.16.cloned.1.call-done = bf16[256,2048]{1,0:T(8,128)(2,1)} async-done(((bf16[1024,2048]{1,0:T(8,128)(2,1)}), bf16[256,2048]{1,0:T(8,128)(2,1)}) %reduce-scatter.16.cloned.1.call-update) | async-done | bytes 1048592 | tf_op jit(solution)/shard_map/reduce_scatter | solution.py:162
  596.2 2.9 fusion.53
  599.1 3.7 fusion.69
  602.9 52.6 %all-gather.23.cloned.1.call-done = bf16[1024,2048]{1,0:T(8,128)(2,1)} async-done(((bf16[256,2048]{1,0:T(8,128)(2,1)}), bf16[1024,2048]{1,0:T(8,128)(2,1)}) %all-gather.23.cloned.1.call-update) | async-done | bytes 4194320 | tf_op jit(solution)/shard_map/all_gather | solution.py:252
  655.6 6.2 multiply_convert_fusion.4
  661.7 104.8 %while.27 = (s32[]{:T(128)}, f32[2,512,8,64]{1,0,3,2:T(2,128)}, f32[2,512,2,64]{1,0,3,2:T(2,128)}, bf16[2,512,2,64]{1,3,2,0:T(8,128)(2,1)}, bf16[2,512,2,64]{1,3...) while((s32[]{:T(128)}, f32[2,512,8,64]{1,0,3,2:T(2,128)}, ...), condition=%wide.region_12.13_spmd, body=%wide.region_10.12_spmd.sunk | while | flops 1365045760 | bytes 140994448 | solution.py:260
  665.3 5.3 fusion.169
  670.6 8.1 fusion.170
  682.6 19.7 %dynamic_update_slice.70 = f32[2,512,8,64]{1,0,3,2:T(2,128)} dynamic-update-slice(f32[2,512,8,64]{1,0,3,2:T(2,128)} %get-tuple-element.382, f32[1,512,8,64]{1,0,3,2:T(1,128)S(1)} %copy.94, s32[]{:T(128)} %get-tuple-element.381, s32[]{:T(128)} %constant.118.clone.1..sunk, s32[]{:T(128)} %constant.118.clone.1..sunk, s32[]{:T(128)} %constant.118.clone.1..sunk) | dynamic-update-slice | bytes 2097156 | tf_op jit(solution)/shard_map/while/body/jit(dynamic_update_index_in_dim)/dynamic_update_slice | solution.py:260
  702.2 3.6 fusion.171
  708.6 5.6 fusion.172
  717.6 5.3 fusion.169
  723.0 8.1 fusion.170
  734.9 19.7 %dynamic_update_slice.70 = f32[2,512,8,64]{1,0,3,2:T(2,128)} dynamic-update-slice(f32[2,512,8,64]{1,0,3,2:T(2,128)} %get-tuple-element.382, f32[1,512,8,64]{1,0,3,2:T(1,128)S(1)} %copy.94, s32[]{:T(128)} %get-tuple-element.381, s32[]{:T(128)} %constant.118.clone.1..sunk, s32[]{:T(128)} %constant.118.clone.1..sunk, s32[]{:T(128)} %constant.118.clone.1..sunk) | dynamic-update-slice | bytes 2097156 | tf_op jit(solution)/shard_map/while/body/jit(dynamic_update_index_in_dim)/dynamic_update_slice | solution.py:260
  754.5 3.6 fusion.171
  760.9 5.6 fusion.172
  772.5 4.3 convolution_convert_fusion.6
  776.9 14.1 %convolution_convert_fusion.1 = bf16[2048,2048]{1,0:T(8,128)(2,1)} fusion(bf16[1024,2048]{1,0:T(8,128)(2,1)} %all-gather.15.cloned.1.call-done, bf16[1024,2048]{1,0:T(8,128)(2,1)} %get-tuple-element.210), kind=kOutput, calls=%fused_computation.70 | convolution fusion | flops 8594128896 | bytes 16777216 | tf_op jit(solution)/shard_map/dot_general | solution.py:95
  791.1 14.1 %convolution_convert_fusion = bf16[2048,2048]{1,0:T(8,128)(2,1)} fusion(bf16[1024,2048]{1,0:T(8,128)(2,1)} %all-gather.15.cloned.1.call-done, bf16[1024,2048]{1,0:T(8,128)(2,1)} %get-tuple-element.211), kind=kOutput, calls=%fused_computation.69 | convolution fusion | flops 8594128896 | bytes 16777216 | tf_op jit(solution)/shard_map/dot_general | solution.py:95
  805.6 14.0 %convert_bitcast_fusion = bf16[2048,2048]{0,1:T(8,128)(2,1)} fusion(bf16[1024,2048]{1,0:T(8,128)(2,1)} %get-tuple-element.212, bf16[1024,2048]{1,0:T(8,128)(2,1)} %all-gather.21.cloned.1.call-done), kind=kOutput, calls=%fused_computation.61 | convolution fusion | flops 8594128896 | bytes 16777216 | tf_op jit(solution)/shard_map/dot_general | solution.py:95
  819.7 6.4 convolution_convert_fusion.4
  830.1 3.8 convolution_convert_fusion.5
  838.2 3.3 add_convert_fusion
  841.5 14.3 %convolution_convert_fusion.2 = bf16[1024,2048]{1,0:T(8,128)(2,1)} fusion(bf16[1024,2048]{1,0:T(8,128)(2,1)} %get-tuple-element.212, bf16[2048,2048]{1,0:T(8,128)(2,1)} %all-gather.19.cloned.1.call-done), kind=kOutput, calls=%fused_computation.77 | convolution fusion | flops 8592031744 | bytes 16777216 | tf_op jit(solution)/shard_map/dot_general | solution.py:101
  858.8 66.7 %reduce-scatter.28.cloned.1.call-done = bf16[256,2048]{1,0:T(8,128)(2,1)} async-done(((bf16[2048,2048]{1,0:T(8,128)(2,1)}), bf16[256,2048]{1,0:T(8,128)(2,1)}) %reduce-scatter.28.cloned.1.call-update) | async-done | bytes 1048592 | tf_op jit(solution)/shard_map/reduce_scatter | solution.py:162
  925.5 2.8 convert_element_type.184
  928.3 87.4 %reduce-scatter.30.cloned.1.call-done = bf16[256,2048]{1,0:T(8,128)(2,1)} async-done(((bf16[2048,2048]{1,0:T(8,128)(2,1)}), bf16[256,2048]{1,0:T(8,128)(2,1)}) %reduce-scatter.30.cloned.1.call-update) | async-done | bytes 1048592 | tf_op jit(solution)/shard_map/reduce_scatter | solution.py:162
  1015.7 2.8 convert_element_type.186
  1018.5 87.3 %reduce-scatter.32.cloned.1.call-done = bf16[256,2048]{0,1:T(8,128)(2,1)} async-done(((bf16[2048,2048]{0,1:T(8,128)(2,1)}), bf16[256,2048]{0,1:T(8,128)(2,1)}) %reduce-scatter.32.cloned.1.call-update) | async-done | bytes 1048592 | tf_op jit(solution)/shard_map/reduce_scatter | solution.py:162
  1105.8 2.6 copy.57
  1108.4 34.2 %reduce-scatter.26.cloned.1.call-done = bf16[256,512]{1,0:T(8,128)(2,1)} async-done(((bf16[2048,512]{1,0:T(8,128)(2,1)}), bf16[256,512]{1,0:T(8,128)(2,1)}) %reduce-scatter.26.cloned.1.call-update) | async-done | bytes 262160 | tf_op jit(solution)/shard_map/reduce_scatter | solution.py:162
  1144.4 35.0 %reduce-scatter.20.cloned.1.call-done = bf16[256,512]{1,0:T(8,128)(2,1)} async-done(((bf16[2048,512]{1,0:T(8,128)(2,1)}), bf16[256,512]{1,0:T(8,128)(2,1)}) %reduce-scatter.20.cloned.1.call-update) | async-done | bytes 262160 | tf_op jit(solution)/shard_map/reduce_scatter | solution.py:162
  1181.2 52.3 %reduce-scatter.18.cloned.1.call-done = bf16[256,2048]{1,0:T(8,128)(2,1)} async-done(((bf16[1024,2048]{1,0:T(8,128)(2,1)}), bf16[256,2048]{1,0:T(8,128)(2,1)}) %reduce-scatter.18.cloned.1.call-update) | async-done | bytes 1048592 | tf_op jit(solution)/shard_map/reduce_scatter | solution.py:162
  1235.4 39.8 %all-reduce = (f32[2048]{0:T(1024)}, f32[2048]{0:T(1024)}) all-reduce(f32[2048]{0:T(1024)S(1)} %get-tuple-element.166, f32[2048]{0:T(1024)S(1)} %copy-done.31), channel_id=1, replica_groups=mesh['dp'=8,'tensor'=4] {'dp','tensor'}, use_global_device_ids=true, to_apply=%region_23.24 | all-reduce | flops 4096 | bytes 32768 | tf_op jit(solution)/shard_map/psum | solution.py:296
  1275.2 14.2 %reduce-scatter.14.cloned.1.call-done = bf16[256,2048]{1,0:T(8,128)(2,1)} async-done(((bf16[1024,2048]{1,0:T(8,128)(2,1)}), bf16[256,2048]{1,0:T(8,128)(2,1)}) %reduce-scatter.14.cloned.1.call-update) | async-done | bytes 1048592 | tf_op jit(solution)/shard_map/reduce_scatter | solution.py:162
  1289.4 4.4 fusion.48
  (255 shorter events, 84.0 us)
Async XLA Ops:
  7.2 7.2 copy-start.29
  7.2 26.0 %copy-start.30 = (bf16[256,128]{1,0:T(8,128)(2,1)S(1)}, bf16[256,128]{1,0:T(8,128)(2,1)}, u32[]{:S(2)}) copy-start(bf16[256,128]{1,0:T(8,128)(2,1)} %param.20) | copy-start | bytes 196612
  7.2 44.3 %copy-start.36 = (s32[1024]{0:T(1024)S(1)}, s32[1024]{0:T(1024)}, u32[]{:S(2)}) copy-start(s32[1024]{0:T(1024)} %param.26) | copy-start | bytes 12292
  7.2 44.3 %all-gather.11.cloned.1.call-start = ((), (), s32[]{:S(2)}) async-start(), calls=%async_computation.12 | async-start | bytes 2359296 | tf_op jit(solution)/shard_map/all_gather | solution.py:182
  7.9 93.9 %all-gather.9.cloned.1.call-start = ((), (), s32[]{:S(2)}) async-start(), calls=%async_computation.11 | async-start | bytes 5242880 | tf_op jit(solution)/shard_map/all_gather | solution.py:198
  13.2 124.8 %all-gather.13.cloned.1.call-start = ((), (), s32[]{:S(2)}) async-start(), calls=%async_computation.13 | async-start | bytes 2359296 | tf_op jit(solution)/shard_map/all_gather | solution.py:185
  13.9 183.3 %reduce-scatter.12.cloned.1.call-start = ((), (), s32[]{:S(2)}) async-start(), calls=%async_computation.14 | async-start | bytes 5242880 | tf_op jit(solution)/shard_map/reduce_scatter | solution.py:162
  14.3 104.2 %copy-start.14 = (f32[512,64]{0,1:T(8,128)}, f32[512,64]{0,1:T(8,128)S(1)}, u32[]{:S(2)}) copy-start(f32[512,64]{0,1:T(8,128)S(1)} %get-tuple-element.224) | copy-start | bytes 393220
  14.4 104.2 %copy-start.16 = (f32[512,64]{0,1:T(8,128)}, f32[512,64]{0,1:T(8,128)S(1)}, u32[]{:S(2)}) copy-start(f32[512,64]{0,1:T(8,128)S(1)} %get-tuple-element.223) | copy-start | bytes 393220
  33.2 80.8 %copy-start.9 = (bf16[2048,128]{1,0:T(8,128)(2,1)}, bf16[2048,128]{1,0:T(8,128)(2,1)S(1)}, u32[]{:S(2)}) copy-start(bf16[2048,128]{1,0:T(8,128)(2,1)S(1)} %all_gather.32) | copy-start | bytes 1572868
  114.5 4.6 copy-start.20
  144.3 52.9 %copy-start.2 = (bf16[256,2048]{1,0:T(8,128)(2,1)S(1)}, bf16[256,2048]{1,0:T(8,128)(2,1)}, u32[]{:S(2)}) copy-start(bf16[256,2048]{1,0:T(8,128)(2,1)} %param.16) | copy-start | bytes 3145732
  144.3 54.6 %copy-start.26 = (f32[2048]{0:T(1024)S(1)}, f32[2048]{0:T(1024)}, u32[]{:S(2)}) copy-start(f32[2048]{0:T(1024)} %param.22) | copy-start | bytes 24580
  144.3 150.7 %all-gather.21.cloned.1.call-start = ((), (), s32[]{:S(2)}) async-start(), calls=%async_computation.19 | async-start | bytes 5242880 | tf_op jit(solution)/shard_map/all_gather | solution.py:236
  144.9 199.6 %all-gather.19.cloned.1.call-start = ((), (), s32[]{:S(2)}) async-start(), calls=%async_computation.17 | async-start | bytes 9437184 | tf_op jit(solution)/shard_map/all_gather | solution.py:188
  145.5 283.2 %all-gather.17.cloned.1.call-start = ((), (), s32[]{:S(2)}) async-start(), calls=%async_computation.16 | async-start | bytes 9437184 | tf_op jit(solution)/shard_map/all_gather | solution.py:187
  146.3 336.0 %all-gather.15.cloned.1.call-start = ((), (), s32[]{:S(2)}) async-start(), calls=%async_computation.15 | async-start | bytes 5242880 | tf_op jit(solution)/shard_map/all_gather | solution.py:222
  146.3 57.9 %collective-permute-start = (bf16[256,2048]{1,0:T(8,128)(2,1)}, bf16[256,2048]{1,0:T(8,128)(2,1)}, u32[]{:S(2)}, u32[]{:S(2)}) collective-permute-start(bf16[256,2048]{1,0:T(8,128)(2,1)} %param.23), channel_id=1, source_target_pairs={{0,4},{4,8},{8,12},{12,16},{16,20},{20,24},{24,28},{28,0},{1,5},{5... | collective-permute-start | bytes 3145736 | tf_op jit(solution)/shard_map/ppermute | solution.py:34
  198.9 400.3 %copy-start.32 = (f32[256]{0:T(256)}, f32[256]{0:T(256)S(1)}, u32[]{:S(2)}) copy-start(f32[256]{0:T(256)S(1)} %get-tuple-element.228) | copy-start | bytes 3076
  198.9 400.3 %copy-start.38 = (f32[256]{0:T(256)}, f32[256]{0:T(256)S(1)}, u32[]{:S(2)}) copy-start(f32[256]{0:T(256)S(1)} %get-tuple-element.227) | copy-start | bytes 3076
  201.5 394.8 %reduce-scatter.16.cloned.1.call-start = ((), (), s32[]{:S(2)}) async-start(), calls=%async_computation.20 | async-start | bytes 5242880 | tf_op jit(solution)/shard_map/reduce_scatter | solution.py:162
  201.5 24.9 %collective-permute-start.1 = (bf16[256,2048]{1,0:T(8,128)(2,1)}, bf16[256,2048]{1,0:T(8,128)(2,1)}, u32[]{:S(2)}, u32[]{:S(2)}) collective-permute-start(bf16[256,2048]{1,0:T(8,128)(2,1)} %param.23), channel_id=1, source_target_pairs={{0,28},{4,0},{8,4},{12,8},{16,12},{20,16},{24,20},{28,24},{1,29},{... | collective-permute-start | bytes 3145736 | tf_op jit(solution)/shard_map/ppermute | solution.py:39
  204.2 26.0 %collective-permute-start.2 = (bf16[256,2048]{1,0:T(8,128)(2,1)}, bf16[256,2048]{1,0:T(8,128)(2,1)}, u32[]{:S(2)}, u32[]{:S(2)}) collective-permute-start(bf16[256,2048]{1,0:T(8,128)(2,1)} %collective-permute-done), channel_id=1, source_target_pairs={{0,4},{4,8},{8,12},{12,16},{16,20},{20,24},{24,28},{28,0},{1,5},{5... | collective-permute-start | bytes 3145736 | tf_op jit(solution)/shard_map/ppermute | solution.py:34
  226.4 24.1 %collective-permute-start.3 = (bf16[256,2048]{1,0:T(8,128)(2,1)}, bf16[256,2048]{1,0:T(8,128)(2,1)}, u32[]{:S(2)}, u32[]{:S(2)}) collective-permute-start(bf16[256,2048]{1,0:T(8,128)(2,1)} %collective-permute-done.1), channel_id=1, source_target_pairs={{0,28},{4,0},{8,4},{12,8},{16,12},{20,16},{24,20},{28,24},{1,29},{... | collective-permute-start | bytes 3145736 | tf_op jit(solution)/shard_map/ppermute | solution.py:39
  230.2 26.4 %collective-permute-start.4 = (bf16[256,2048]{1,0:T(8,128)(2,1)}, bf16[256,2048]{1,0:T(8,128)(2,1)}, u32[]{:S(2)}, u32[]{:S(2)}) collective-permute-start(bf16[256,2048]{1,0:T(8,128)(2,1)} %collective-permute-done.2), channel_id=1, source_target_pairs={{0,4},{4,8},{8,12},{12,16},{16,20},{20,24},{24,28},{28,0},{1,5},{5... | collective-permute-start | bytes 3145736 | tf_op jit(solution)/shard_map/ppermute | solution.py:34
  250.6 42.3 %collective-permute-start.5 = (bf16[256,2048]{1,0:T(8,128)(2,1)}, bf16[256,2048]{1,0:T(8,128)(2,1)S(1)}, u32[]{:S(2)}, u32[]{:S(2)}) collective-permute-start(bf16[256,2048]{1,0:T(8,128)(2,1)} %collective-permute-done.3), channel_id=1, source_target_pairs={{0,28},{4,0},{8,4},{12,8},{16,12},{20,16},{24,20},{28,24},{1,29},{... | collective-permute-start | bytes 3145736 | tf_op jit(solution)/shard_map/ppermute | solution.py:39
  256.6 37.3 %collective-permute-start.6 = (bf16[256,2048]{1,0:T(8,128)(2,1)}, bf16[256,2048]{1,0:T(8,128)(2,1)S(1)}, u32[]{:S(2)}, u32[]{:S(2)}) collective-permute-start(bf16[256,2048]{1,0:T(8,128)(2,1)} %collective-permute-done.4), channel_id=1, source_target_pairs={{0,4},{4,8},{8,12},{12,16},{16,20},{20,24},{24,28},{28,0},{1,5},{5... | collective-permute-start | bytes 3145736 | tf_op jit(solution)/shard_map/ppermute | solution.py:34
  482.2 15.5 %copy-start.43 = (bf16[1024,2048]{1,0:T(8,128)(2,1)S(1)}, bf16[1024,2048]{1,0:T(8,128)(2,1)}, u32[]{:S(2)}) copy-start(bf16[1024,2048]{1,0:T(8,128)(2,1)} %all-gather.15.cloned.1.call-done) | copy-start | bytes 12582916
  517.4 13.2 %copy-start.45 = (bf16[1024,2048]{1,0:T(8,128)(2,1)S(1)}, bf16[1024,2048]{1,0:T(8,128)(2,1)}, u32[]{:S(2)}) copy-start(bf16[1024,2048]{1,0:T(8,128)(2,1)} %get-tuple-element.210) | copy-start | bytes 12582916
  543.5 59.4 %copy-start.37 = (s32[1024]{0:T(1024)S(1)}, s32[1024]{0:T(1024)}, u32[]{:S(2)}) copy-start(s32[1024]{0:T(1024)} %param.26) | copy-start | bytes 12292
  543.5 112.1 %all-gather.23.cloned.1.call-start = ((), (), s32[]{:S(2)}) async-start(), calls=%async_computation.21 | async-start | bytes 5242880 | tf_op jit(solution)/shard_map/all_gather | solution.py:252
  599.1 62.6 %copy-start.40 = (f32[256]{0:T(256)}, f32[256]{0:T(256)S(1)}, u32[]{:S(2)}) copy-start(f32[256]{0:T(256)S(1)} %broadcast_multiply_fusion.3) | copy-start | bytes 3076
  602.8 253.0 %reduce-scatter.22.cloned.1.call-start = ((), (), s32[]{:S(2)}) async-start(), calls=%async_computation.24 | async-start | bytes 589824 | tf_op jit(solution)/shard_map/reduce_scatter | solution.py:162
  661.7 104.8 %copy-start.15 = (f32[512,64]{0,1:T(8,128)S(1)}, f32[512,64]{0,1:T(8,128)}, u32[]{:S(2)}) copy-start(f32[512,64]{0,1:T(8,128)} %copy-done.14) | copy-start | bytes 393220
  664.9 5.7 copy-start.1
  682.6 23.5 %copy-start.22 = (f32[2,512,2,64]{1,0,3,2:T(2,128)S(1)}, f32[2,512,2,64]{1,0,3,2:T(2,128)}, u32[]{:S(2)}) copy-start(f32[2,512,2,64]{1,0,3,2:T(2,128)} %get-tuple-element.383) | copy-start | bytes 1572868 | tf_op jit(solution)/shard_map/while
  708.5 5.7 copy-start.23
  708.5 5.7 copy-start.5
  708.6 5.7 copy-start.19
  717.2 5.7 copy-start.1
  734.9 23.5 %copy-start.22 = (f32[2,512,2,64]{1,0,3,2:T(2,128)S(1)}, f32[2,512,2,64]{1,0,3,2:T(2,128)}, u32[]{:S(2)}) copy-start(f32[2,512,2,64]{1,0,3,2:T(2,128)} %get-tuple-element.383) | copy-start | bytes 1572868 | tf_op jit(solution)/shard_map/while
  760.9 5.7 copy-start.23
  760.9 5.7 copy-start.5
  760.9 5.7 copy-start.19
  772.0 85.4 %reduce-scatter.24.cloned.1.call-start = ((), (), s32[]{:S(2)}) async-start(), calls=%async_computation.25 | async-start | bytes 589824 | tf_op jit(solution)/shard_map/reduce_scatter | solution.py:162
  776.9 148.6 %reduce-scatter.28.cloned.1.call-start = ((), (), s32[]{:S(2)}) async-start(), calls=%async_computation.27 | async-start | bytes 9437184 | tf_op jit(solution)/shard_map/reduce_scatter | solution.py:162
  791.0 224.7 %reduce-scatter.30.cloned.1.call-start = ((), (), s32[]{:S(2)}) async-start(), calls=%async_computation.28 | async-start | bytes 9437184 | tf_op jit(solution)/shard_map/reduce_scatter | solution.py:162
  805.2 300.7 %reduce-scatter.32.cloned.1.call-start = ((), (), s32[]{:S(2)}) async-start(), calls=%async_computation.29 | async-start | bytes 9437184 | tf_op jit(solution)/shard_map/reduce_scatter | solution.py:162
  819.6 6.5 copy-start.8
  819.7 322.9 %reduce-scatter.26.cloned.1.call-start = ((), (), s32[]{:S(2)}) async-start(), calls=%async_computation.26 | async-start | bytes 2359296 | tf_op jit(solution)/shard_map/reduce_scatter | solution.py:162
  826.1 353.2 %reduce-scatter.20.cloned.1.call-start = ((), (), s32[]{:S(2)}) async-start(), calls=%async_computation.23 | async-start | bytes 2359296 | tf_op jit(solution)/shard_map/reduce_scatter | solution.py:162
  833.9 399.6 %reduce-scatter.18.cloned.1.call-start = ((), (), s32[]{:S(2)}) async-start(), calls=%async_computation.22 | async-start | bytes 5242880 | tf_op jit(solution)/shard_map/reduce_scatter | solution.py:162
  841.5 447.9 %reduce-scatter.14.cloned.1.call-start = ((), (), s32[]{:S(2)}) async-start(), calls=%async_computation.18 | async-start | bytes 5242880 | tf_op jit(solution)/shard_map/reduce_scatter | solution.py:162
  928.3 305.2 %copy-start.3 = (bf16[256,2048]{1,0:T(8,128)(2,1)S(1)}, bf16[256,2048]{1,0:T(8,128)(2,1)}, u32[]{:S(2)}) copy-start(bf16[256,2048]{1,0:T(8,128)(2,1)} %param.16) | copy-start | bytes 3145732
  928.3 305.2 %copy-start.28 = (f32[2048]{0:T(1024)S(1)}, f32[2048]{0:T(1024)}, u32[]{:S(2)}) copy-start(f32[2048]{0:T(1024)} %param.17) | copy-start | bytes 24580
  928.3 305.2 %copy-start.35 = (f32[256]{0:T(256)S(1)}, f32[256]{0:T(256)}, u32[]{:S(2)}) copy-start(f32[256]{0:T(256)} %copy-done.34) | copy-start | bytes 3076
  1018.5 216.9 %copy-start.31 = (f32[2048]{0:T(1024)S(1)}, f32[2048]{0:T(1024)}, u32[]{:S(2)}) copy-start(f32[2048]{0:T(1024)} %get-tuple-element.164) | copy-start | bytes 24580
  1018.5 270.9 %copy-start.6 = (bf16[256,2048]{1,0:T(8,128)(2,1)S(1)}, bf16[256,2048]{1,0:T(8,128)(2,1)}, u32[]{:S(2)}) copy-start(bf16[256,2048]{1,0:T(8,128)(2,1)} %reduce-scatter.12.cloned.1.call-done) | copy-start | bytes 3145732
  1018.5 270.9 %copy-start.7 = (bf16[256,2048]{1,0:T(8,128)(2,1)S(1)}, bf16[256,2048]{1,0:T(8,128)(2,1)}, u32[]{:S(2)}) copy-start(bf16[256,2048]{1,0:T(8,128)(2,1)} %param.27) | copy-start | bytes 3145732
  1018.5 270.9 %copy-start.27 = (f32[2048]{0:T(1024)S(1)}, f32[2048]{0:T(1024)}, u32[]{:S(2)}) copy-start(f32[2048]{0:T(1024)} %param.22) | copy-start | bytes 24580
  1018.5 270.9 %copy-start.33 = (f32[256]{0:T(256)S(1)}, f32[256]{0:T(256)}, u32[]{:S(2)}) copy-start(f32[256]{0:T(256)} %copy-done.32) | copy-start | bytes 3076
  1018.5 270.9 %copy-start.39 = (f32[256]{0:T(256)S(1)}, f32[256]{0:T(256)}, u32[]{:S(2)}) copy-start(f32[256]{0:T(256)} %copy-done.38) | copy-start | bytes 3076
  1018.5 270.9 %copy-start.41 = (f32[256]{0:T(256)S(1)}, f32[256]{0:T(256)}, u32[]{:S(2)}) copy-start(f32[256]{0:T(256)} %copy-done.40) | copy-start | bytes 3076
  1018.5 270.9 %copy-start.42 = (f32[256]{0:T(256)S(1)}, f32[256]{0:T(256)}, u32[]{:S(2)}) copy-start(f32[256]{0:T(256)} %get-tuple-element.225) | copy-start | bytes 3076
  (16 other events, 42.8 us)
Sparse Core Ops, SparseCore 0:
  9.6 37.0 all-gather.10
  49.1 52.6 all-gather.8
  103.4 29.1 all-gather.12
  144.5 52.6 reduce-scatter.11
  198.9 52.5 all-gather.20
  252.9 91.5 all-gather.18
  346.1 82.5 all-gather.16
  431.2 51.0 all-gather.14
  543.6 52.5 reduce-scatter.15
  603.0 52.5 all-gather.22
  772.1 31.2 reduce-scatter.21
  806.1 29.4 reduce-scatter.23
  837.9 87.6 reduce-scatter.27
  927.7 87.9 reduce-scatter.29
  1017.8 87.9 reduce-scatter.31
  1108.0 34.5 reduce-scatter.25
  1144.7 34.6 reduce-scatter.19
  1182.2 51.2 reduce-scatter.17
  1236.5 52.8 reduce-scatter.13
